TPU v7x, 256 devices: a whole 4x4x8 slice. The times are simulated.
256 devices in a mesh: gx: 16 (over z, core), gy: 4 (over x), gz: 4 (over y).
Axes of the slice: x: 4, y: 4, z: 8, core: 2. Of those that a mesh axis runs over, the one named last changes fastest.
Arguments:
- velocity: float32 [3, 1024, 128, 512], P(None, 'gx', 'gz', 'gy'), may hold values from -6 to 6
- tile_turbine: int32 [16, 4, 4, 2], P('gx', 'gz', 'gy'), may hold values from 0 to 63
- tile_plane: int32 [16, 4, 4, 2], P('gx', 'gz', 'gy'), may hold values from 0 to 63
- tile_weight: bfloat16 [16, 4, 4, 2, 384, 4096], P('gx', 'gz', 'gy'), may hold values from -0.09375 to 0.09375
- chord: float32 [64, 384], replicated, may hold values from 0.25 to 1
Outputs:
- predicted: float32 [3, 1024, 128, 512], P(None, 'gx', 'gz', 'gy')
- forces: float32 [64, 1152], replicated
All inputs are finite; a program needn't handle non-finite values.
Results may differ from a plain program's by a relative error of at most 0.0032.
Values sent between devices are 32-bit elements; how exact they have to be, the bound alone decides.
No kernel may reach another device: no remote copies, remote signals or barrier semaphores. Data moves between devices by JAX's collectives and lax.ppermute only.
A program may use at most 128 MiB of HBM per device.

v0:
```python
import jax
import jax.numpy as jnp
from jax import lax
from jax.sharding import PartitionSpec as P

DIRS = (-3, -1, -2)


def padded_2(block, sides, width):
    for axis, dim in sides:
        count = lax.axis_size(axis)
        forward = [(i, i + 1) for i in range(count - 1)]
        backward = [(target, source) for source, target in forward]
        low = lax.ppermute(
            lax.slice_in_dim(block, block.shape[dim] - width, None, axis=dim), axis, forward
        )
        high = lax.ppermute(lax.slice_in_dim(block, 0, width, axis=dim), axis, backward)
        block = jnp.concatenate([low, block, high], axis=dim)
    return block


def shifted(p, axis, step):
    idx = [slice(1, -1), slice(1, -1), slice(1, -1)]
    idx[axis + 3] = slice(1 + step, p.shape[axis] - 1 + step)
    lead = [slice(None)] * (p.ndim - 3)
    return p[tuple(lead + idx)]


def strain_viscosity(p):
    grads = [
        [0.5 * (shifted(p[c], DIRS[d], 1) - shifted(p[c], DIRS[d], -1)) for d in range(3)]
        for c in range(3)
    ]
    total = jnp.zeros_like(grads[0][0])
    for c in range(3):
        for d in range(3):
            strain = 0.5 * (grads[c][d] + grads[d][c])
            total = total + strain * strain
    return 0.05 + 1.0 * jnp.sqrt(2.0 * total + 1e-06)


def advance(padded, nu_padded):
    nu_here = shifted(nu_padded, -1, 0)
    result = []
    for c in range(3):
        center = shifted(padded[c], -1, 0)
        advect = jnp.zeros_like(center)
        spread = jnp.zeros_like(center)
        for d in range(3):
            upper = shifted(padded[c], DIRS[d], 1)
            lower = shifted(padded[c], DIRS[d], -1)
            advect = advect + shifted(padded[d], -1, 0) * 0.5 * (upper - lower)
            nu_up = 0.5 * (nu_here + shifted(nu_padded, DIRS[d], 1))
            nu_low = 0.5 * (nu_here + shifted(nu_padded, DIRS[d], -1))
            spread = spread + nu_up * (upper - center) - nu_low * (center - lower)
        result.append(center + 0.25 * (spread - advect))
    return jnp.stack(result)


def actuate(velocity_probe, coef):
    rows = velocity_probe.shape[0]
    parts = velocity_probe.reshape(rows, 3, -1)
    magnitude = jnp.sqrt(jnp.sum(parts * parts, axis=1) + 1e-06)
    return (-2.0 * coef[:, None, :] * magnitude[:, None, :] * parts).reshape(rows, -1)


def body(velocity, tile_turbine, tile_plane, tile_weight, chord):
    cx = velocity.shape[1]
    vertical_coord = velocity.shape[2]
    spanwise_coord = velocity.shape[3]
    tile_count = tile_turbine.shape[3]
    actuator_count = tile_weight.shape[4]
    nturb = chord.shape[0]
    turbine_list = tile_turbine.reshape(tile_count)
    rotor_planes = tile_plane.reshape(tile_count)
    spread_weights = tile_weight.reshape(
        tile_count, actuator_count, vertical_coord * spanwise_coord
    )
    flat = velocity.reshape(3, cx, vertical_coord * spanwise_coord)
    picks = (rotor_planes[:, None] == jnp.arange(cx, dtype=jnp.int32)[None, :]).astype(jnp.float32)
    tiles = jnp.einsum("sx,cxq->scq", picks, flat, precision=lax.Precision.HIGHEST).astype(
        jnp.bfloat16
    )
    block_local = jnp.einsum(
        "spq,scq->scp", spread_weights, tiles, preferred_element_type=jnp.float32
    )
    owning_block = (turbine_list[:, None] == jnp.arange(nturb, dtype=jnp.int32)[None, :]).astype(
        jnp.float32
    )
    partial_sample = jnp.einsum(
        "yr,yw->rw",
        owning_block,
        block_local.reshape(tile_count, -1),
        precision=lax.Precision.HIGHEST,
    )
    rows = lax.axis_size("gx")
    per_row = nturb // rows
    received = lax.all_to_all(
        partial_sample.reshape(rows, per_row, -1), "gx", split_axis=0, concat_axis=0, tiled=True
    )
    owned = lax.psum(jnp.sum(received, axis=0), ("gy", "gz"))
    owned_coef = lax.dynamic_slice_in_dim(chord, lax.axis_index("gx") * per_row, per_row, 0)
    forces = lax.all_gather(actuate(owned, owned_coef), "gx", axis=0, tiled=True)
    tile_force = jnp.dot(owning_block, forces, precision=lax.Precision.HIGHEST).astype(jnp.bfloat16)
    forces_sent = jnp.einsum(
        "axz,ahx->ahz",
        spread_weights,
        tile_force.reshape(tile_count, 3, actuator_count),
        preferred_element_type=jnp.float32,
    )
    impulse = jnp.einsum(
        "sx,scq->cxq", picks, forces_sent, precision=lax.Precision.HIGHEST
    ).reshape(3, cx, vertical_coord, spanwise_coord)
    padded = padded_2(velocity, (("gx", 1), ("gy", 3), ("gz", 2)), 1)
    viscosity = strain_viscosity(padded)
    nu_padded = padded_2(viscosity, (("gx", 0), ("gy", 2), ("gz", 1)), 1)
    predicted = advance(padded, nu_padded) + impulse
    return (predicted, forces)


def solution(mesh):
    placed = (
        P(None, "gx", "gz", "gy"),
        P("gx", "gz", "gy", None),
        P("gx", "gz", "gy", None),
        P("gx", "gz", "gy", None, None, None),
        P(),
    )
    return jax.shard_map(
        body,
        mesh=mesh,
        in_specs=placed,
        out_specs=(P(None, "gx", "gz", "gy"), P()),
        check_vma=False,
    )
```

profile of v0, /device:TPU:1, one launch (start us, length us, event | category | flops | bytes accessed | tf_op | source)
XLA Modules:
  0.0 237.4 jit_solution(2430142811792057786)
XLA Ops:
  0.6 0.8 fusion.31
  1.5 4.9 %collective-permute-start = (f32[3,1,32,128]{3,2,1,0:T(8,128)S(1)}, f32[3,1,32,128]{3,2,1,0:T(8,128)S(1)}, u32[]{:S(2)}, u32[]{:S(2)}) collective-permute-start(f32[3,1,32,128]{3,2,1,0:T(8,128)S(1)} %get-tuple-element.16), channel_id=1, source_target_pairs={{0,16},{16,32},{32,48},{48,64},{64,80},{80,96},{96,112},{112,128},... | collective-permute-start | bytes 147464 | tf_op jit(solution)/shard_map/ppermute | solution.py:14
  6.4 1.9 collective-permute-start.1
  8.3 2.2 constant_dynamic-update-slice_fusion.1
  10.5 1.3 collective-permute-done.1
  11.8 3.9 %fusion.30 = (f32[3,66,32,1]{3,2,1,0:T(8,128)}, f32[3,66,32,1]{3,2,1,0:T(8,128)}) fusion(f32[3,66,32,128]{3,2,1,0:T(8,128)S(1)} %constant_dynamic-update-slice_fusion), kind=kLoop, calls=%fused_computation.87 | loop fusion | bytes 101376 | tf_op jit(solution)/shard_map/slice | solution.py:15
  15.7 2.8 %copy.29 = f32[3,66,32,1]{1,2,3,0:T(8,128)S(1)} copy(f32[3,66,32,1]{3,2,1,0:T(8,128)} %get-tuple-element.13) | data formatting | bytes 50688 | tf_op jit(solution)/shard_map/slice | solution.py:15
  18.5 3.1 %collective-permute-start.2 = (f32[3,66,32,1]{1,2,3,0:T(8,128)S(1)}, f32[3,66,32,1]{1,2,3,0:T(8,128)S(1)}, u32[]{:S(2)}, u32[]{:S(2)}) collective-permute-start(f32[3,66,32,1]{1,2,3,0:T(8,128)S(1)} %copy.29), channel_id=1, source_target_pairs={{0,4},{4,8},{8,12},{1,5},{5,9},{9,13},{2,6},{6,10},{10,14},{3,7},{... | collective-permute-start | bytes 76040 | tf_op jit(solution)/shard_map/ppermute | solution.py:14
  21.6 2.8 %copy.30 = f32[3,66,32,1]{1,2,3,0:T(8,128)S(1)} copy(f32[3,66,32,1]{3,2,1,0:T(8,128)} %get-tuple-element.14) | data formatting | bytes 50688 | tf_op jit(solution)/shard_map/slice | solution.py:17
  24.4 1.3 collective-permute-start.3
  25.7 4.6 %reshape.47 = f32[3,64,4096]{2,1,0:T(8,128)} reshape(f32[3,64,32,128]{3,2,1,0:T(8,128)} %param.5) | data formatting | bytes 6291456 | tf_op jit(solution)/shard_map/reshape | solution.py:79
  30.3 2.7 %copy.31 = f32[3,66,32,1]{3,2,1,0:T(8,128)} copy(f32[3,66,32,1]{1,2,3,0:T(8,128)S(1)} %collective-permute-done.2) | data formatting | bytes 50688 | tf_op jit(solution)/shard_map/ppermute | solution.py:14
  33.0 2.7 %copy.32 = f32[3,66,32,1]{3,2,1,0:T(8,128)} copy(f32[3,66,32,1]{1,2,3,0:T(8,128)S(1)} %collective-permute-done.3) | data formatting | bytes 50688 | tf_op jit(solution)/shard_map/ppermute | solution.py:17
  35.7 3.4 %pad_maximum_fusion.22 = (f32[3,66,1,130]{3,2,1,0:T(1,128)S(1)}, f32[3,66,1,130]{3,2,1,0:T(1,128)S(1)}) fusion(f32[3,66,32,1]{3,2,1,0:T(8,128)} %copy.32, f32[3,66,32,128]{3,2,1,0:T(8,128)S(1)} %constant_dynamic-update-slice_fusion, f32[3,66,32,1]{3,2,1,0:T(8,128)} %copy.31), kind=kLoop, calls=%fused_computation.60 | loop fusion | flops 102960 | bytes 3500640 | tf_op jit(solution)/shard_map/slice | solution.py:15
  39.1 3.3 %collective-permute-start.4 = (f32[3,66,1,130]{3,2,1,0:T(1,128)S(1)}, f32[3,66,1,130]{3,2,1,0:T(1,128)S(1)}, u32[]{:S(2)}, u32[]{:S(2)}) collective-permute-start(f32[3,66,1,130]{3,2,1,0:T(1,128)S(1)} %get-tuple-element.6), channel_id=1, source_target_pairs={{0,1},{1,2},{2,3},{4,5},{5,6},{6,7},{8,9},{9,10},{10,11},{12,13},{... | collective-permute-start | bytes 308888 | tf_op jit(solution)/shard_map/ppermute | solution.py:14
  42.5 1.3 collective-permute-start.5
  43.8 1.1 convolution_convert_fusion
  44.9 0.9 collective-permute-done.4
  45.8 4.1 %collective-permute-done.5 = f32[3,66,1,130]{3,2,1,0:T(1,128)S(1)} collective-permute-done((f32[3,66,1,130]{3,2,1,0:T(1,128)S(1)}, f32[3,66,1,130]{3,2,1,0:T(1,128)S(1)}, u32[]{:S(2)}, u32[]{:S(2)}) %collective-permute-start.5) | collective-permute-done | bytes 102992 | tf_op jit(solution)/shard_map/ppermute | solution.py:17
  49.9 4.0 %pad_maximum_fusion = f32[3,66,34,130]{3,2,1,0:T(8,128)S(1)} fusion(f32[3,66,1,130]{3,2,1,0:T(1,128)S(1)} %collective-permute-done.5, f32[3,66,32,1]{3,2,1,0:T(8,128)S(1)} %copy-done.7, f32[3,66,32,128]{3,2,1,0:T(8,128)S(1)} %constant_dynamic-update-slice_fusion, f32[3,66,32,1]{3,2,1,0:T(8,128)S(1)} %copy-done.6, f32[3,66,1,130]{3,2,1,0:T(1,128)S(1)} %collective-permute-done.4), kind=kLoop, calls=%fused_computation | loop fusion | flops 3500640 | bytes 7001280 | tf_op jit(solution)/shard_map/concatenate | solution.py:18
  53.9 0.5 slice_bitcast_fusion.1
  54.5 4.8 %sqrt_add_fusion = f32[64,32,128]{2,1,0:T(8,128)S(1)} fusion(f32[66,34,130]{2,1,0:T(8,128)S(1)} %get-tuple-element.10, f32[66,34,130]{2,1,0:T(8,128)S(1)} %get-tuple-element.8, f32[66,34,130]{2,1,0:T(8,128)S(1)} %get-tuple-element.9), kind=kLoop, calls=%fused_computation.45 | loop fusion | flops 9961472 | bytes 19922944 | tf_op jit(solution)/shard_map/add | solution.py:39
  59.3 1.9 collective-permute-start.6
  61.2 5.5 %collective-permute-start.7 = (f32[1,32,128]{2,1,0:T(8,128)S(1)}, f32[1,32,128]{2,1,0:T(8,128)S(1)}, u32[]{:S(2)}, u32[]{:S(2)}) collective-permute-start(f32[1,32,128]{2,1,0:T(8,128)S(1)} %get-tuple-element.19), channel_id=1, source_target_pairs={{0,16},{16,32},{32,48},{48,64},{64,80},{80,96},{96,112},{112,128},... | collective-permute-start | bytes 49160 | tf_op jit(solution)/shard_map/ppermute | solution.py:14
  66.8 4.5 %fusion.2 = f32[2,3,384]{2,1,0:T(4,128)S(1)} fusion(bf16[1,1,1,2,384,4096]{5,4,3,2,1,0:T(8,128)(2,1)} %param.8, bf16[2,3,4096]{2,0,1:T(2,128)(2,1)S(1)} %convolution_convert_fusion), kind=kOutput, calls=%fused_computation.3 | convolution fusion | flops 18874368 | bytes 6349824 | tf_op jit(solution)/shard_map/spq,scq->scp/dot_general | solution.py:84
  71.4 1.7 fusion.32
  73.1 1.9 copy.33
  75.0 1.3 collective-permute-start.8
  76.3 1.9 copy.35
  78.2 4.6 %collective-permute-start.9 = (f32[66,32,1]{0,1,2:T(8,128)S(1)}, f32[66,32,1]{0,1,2:T(8,128)S(1)}, u32[]{:S(2)}, u32[]{:S(2)}) collective-permute-start(f32[66,32,1]{0,1,2:T(8,128)S(1)} %copy.35), channel_id=1, source_target_pairs={{0,4},{4,8},{8,12},{1,5},{5,9},{9,13},{2,6},{6,10},{10,14},{3,7},{... | collective-permute-start | bytes 25352 | tf_op jit(solution)/shard_map/ppermute | solution.py:14
  82.8 1.9 copy.34
  84.7 1.9 copy.36
  86.6 1.9 pad_maximum_fusion.23
  88.5 1.3 collective-permute-start.10
  89.8 4.0 %collective-permute-start.11 = (f32[66,1,130]{2,1,0:T(1,128)S(1)}, f32[66,1,130]{2,1,0:T(1,128)S(1)}, u32[]{:S(2)}, u32[]{:S(2)}) collective-permute-start(f32[66,1,130]{2,1,0:T(1,128)S(1)} %get-tuple-element.11), channel_id=1, source_target_pairs={{0,1},{1,2},{2,3},{4,5},{5,6},{6,7},{8,9},{9,10},{10,11},{12,13},{... | collective-permute-start | bytes 102968 | tf_op jit(solution)/shard_map/ppermute | solution.py:14
  94.2 0.8 copy.40
  95.1 7.6 %all-to-all-start = ((f32[16,4,1152]{2,1,0:T(4,128)}), f32[16,4,1152]{2,1,0:T(4,128)S(1)}, u32[]{:S(2)}, u32[]{:S(2)}) async-start(f32[16,4,1152]{2,1,0:T(4,128)} %copy.40), calls=%async_computation | async-start | bytes 589824 | tf_op jit(solution)/shard_map/all_to_all | solution.py:98
  102.7 17.9 %add_bitcast_fusion.2 = f32[1,64,32,128]{3,2,1,0:T(8,128)} fusion(f32[66,34,130]{2,1,0:T(8,128)} %copy-done.2, f32[66,34,130]{2,1,0:T(8,128)S(1)} %get-tuple-element.8, f32[66,34,130]{2,1,0:T(8,128)} %copy-done, f32[64,32,128]{2,1,0:T(8,128)} %copy-done.4, f32[1,32,128]{2,1,0:T(8,128)S(1)} %collective-permute-done.6, ...), kind=kLoop, calls=%fused_computation.44 | loop fusion | flops 15990784 | bytes 11652640 | tf_op jit(solution)/shard_map/stack | solution.py:57
  120.7 7.1 %add_bitcast_fusion.1 = f32[1,64,32,128]{3,2,1,0:T(8,128)} fusion(f32[66,34,130]{2,1,0:T(8,128)S(1)} %get-tuple-element.8, f32[66,34,130]{2,1,0:T(8,128)S(1)} %copy-done.3, f32[66,34,130]{2,1,0:T(8,128)S(1)} %copy-done.1, f32[64,32,128]{2,1,0:T(8,128)S(1)} %copy-done.5, f32[1,32,128]{2,1,0:T(8,128)S(1)} %collective-permute-done.6, ...), kind=kLoop, calls=%fused_computation.43 | loop fusion | flops 15990784 | bytes 11652640 | tf_op jit(solution)/shard_map/stack | solution.py:57
  127.9 7.1 %add_bitcast_fusion = f32[1,64,32,128]{3,2,1,0:T(8,128)} fusion(f32[66,34,130]{2,1,0:T(8,128)S(1)} %copy-done.1, f32[66,34,130]{2,1,0:T(8,128)S(1)} %copy-done.3, f32[66,34,130]{2,1,0:T(8,128)S(1)} %get-tuple-element.8, f32[64,32,128]{2,1,0:T(8,128)S(1)} %copy-done.5, f32[1,32,128]{2,1,0:T(8,128)S(1)} %collective-permute-done.6, ...), kind=kLoop, calls=%fused_computation.42 | loop fusion | flops 15990784 | bytes 11652640 | tf_op jit(solution)/shard_map/stack | solution.py:57
  135.0 59.5 %psum.7 = f32[4,1152]{1,0:T(4,128)S(1)} all-reduce(f32[4,1152]{1,0:T(4,128)S(1)} %reduce_sum.18), channel_id=1, replica_groups=mesh['gx'=16,'gy'=4,'gz'=4] {'gy','gz'}, use_global_device_ids=true, to_apply=%region_1.0 | all-reduce | flops 4608 | bytes 36864 | tf_op jit(solution)/shard_map/psum | solution.py:101
  194.5 0.7 sqrt_multiply_fusion
  195.3 32.2 %all-gather = f32[16,4,1152]{2,1,0:T(4,128)S(1)} all-gather(f32[1,4,1152]{2,1,0:T(4,128)S(1)} %multiply_bitcast_fusion), channel_id=1, replica_groups=mesh['gx'=16,'gy'=4,'gz'=4] {'gx'}, dimensions={0}, use_global_device_ids=true | all-gather | bytes 313344 | tf_op jit(solution)/shard_map/all_gather | solution.py:103
  227.9 3.7 %fusion = f32[2,3,4096]{2,1,0:T(4,128)S(1)} fusion(bf16[2,3,384]{2,1,0:T(4,128)(2,1)S(1)} %reshape.50, bf16[1,1,1,2,384,4096]{5,4,3,2,1,0:T(8,128)(2,1)} %param.8), kind=kOutput, calls=%fused_computation.1 | convolution fusion | flops 18874368 | bytes 6394368 | tf_op jit(solution)/shard_map/axz,ahx->ahz/dot_general | solution.py:105
  231.6 1.5 fusion.16
  233.2 0.5 copy.42
  233.7 0.6 copy-done.11
  235.0 2.4 %bitcast_add_fusion = f32[3,64,32,128]{3,2,1,0:T(8,128)} fusion(f32[1,64,32,128]{3,2,1,0:T(8,128)S(1)} %copy-done.13, f32[1,64,32,128]{3,2,1,0:T(8,128)S(1)} %copy-done.12, f32[1,64,32,128]{3,2,1,0:T(8,128)S(1)} %copy-done.11, f32[3,64,32,128]{3,2,1,0:T(8,128)S(1)} %bitcast.42), kind=kLoop, calls=%fused_computation.6 | loop fusion | flops 2359296 | bytes 9437184 | tf_op jit(solution)/shard_map/add | solution.py:117
  (58 shorter events, 1.7 us)
Async XLA Ops:
  1.5 6.9 %collective-permute-start = (f32[3,1,32,128]{3,2,1,0:T(8,128)S(1)}, f32[3,1,32,128]{3,2,1,0:T(8,128)S(1)}, u32[]{:S(2)}, u32[]{:S(2)}) collective-permute-start(f32[3,1,32,128]{3,2,1,0:T(8,128)S(1)} %get-tuple-element.16), channel_id=1, source_target_pairs={{0,16},{16,32},{32,48},{48,64},{64,80},{80,96},{96,112},{112,128},... | collective-permute-start | bytes 147464 | tf_op jit(solution)/shard_map/ppermute | solution.py:14
  6.4 5.4 %collective-permute-start.1 = (f32[3,1,32,128]{3,2,1,0:T(8,128)S(1)}, f32[3,1,32,128]{3,2,1,0:T(8,128)S(1)}, u32[]{:S(2)}, u32[]{:S(2)}) collective-permute-start(f32[3,1,32,128]{3,2,1,0:T(8,128)S(1)} %get-tuple-element.15), channel_id=1, source_target_pairs={{16,0},{32,16},{48,32},{64,48},{80,64},{96,80},{112,96},{128,112},... | collective-permute-start | bytes 147464 | tf_op jit(solution)/shard_map/ppermute | solution.py:17
  18.5 11.8 %collective-permute-start.2 = (f32[3,66,32,1]{1,2,3,0:T(8,128)S(1)}, f32[3,66,32,1]{1,2,3,0:T(8,128)S(1)}, u32[]{:S(2)}, u32[]{:S(2)}) collective-permute-start(f32[3,66,32,1]{1,2,3,0:T(8,128)S(1)} %copy.29), channel_id=1, source_target_pairs={{0,4},{4,8},{8,12},{1,5},{5,9},{9,13},{2,6},{6,10},{10,14},{3,7},{... | collective-permute-start | bytes 76040 | tf_op jit(solution)/shard_map/ppermute | solution.py:14
  24.4 8.6 %collective-permute-start.3 = (f32[3,66,32,1]{1,2,3,0:T(8,128)S(1)}, f32[3,66,32,1]{1,2,3,0:T(8,128)S(1)}, u32[]{:S(2)}, u32[]{:S(2)}) collective-permute-start(f32[3,66,32,1]{1,2,3,0:T(8,128)S(1)} %copy.30), channel_id=1, source_target_pairs={{4,0},{8,4},{12,8},{5,1},{9,5},{13,9},{6,2},{10,6},{14,10},{7,3},{... | collective-permute-start | bytes 76040 | tf_op jit(solution)/shard_map/ppermute | solution.py:17
  35.7 8.1 %copy-start.10 = (f32[3,64,4096]{2,1,0:T(8,128)S(1)}, f32[3,64,4096]{2,1,0:T(8,128)}, u32[]{:S(2)}) copy-start(f32[3,64,4096]{2,1,0:T(8,128)} %reshape.47) | copy-start | bytes 9437188
  35.7 8.1 %copy-start.16 = (s32[1,1,1,2]{3,2,1,0:T(1,128)S(1)}, s32[1,1,1,2]{3,2,1,0:T(1,128)}, u32[]{:S(2)}) copy-start(s32[1,1,1,2]{3,2,1,0:T(1,128)} %param.7) | copy-start | bytes 28
  35.7 14.2 %copy-start.6 = (f32[3,66,32,1]{3,2,1,0:T(8,128)S(1)}, f32[3,66,32,1]{3,2,1,0:T(8,128)}, u32[]{:S(2)}) copy-start(f32[3,66,32,1]{3,2,1,0:T(8,128)} %copy.31) | copy-start | bytes 76036
  35.7 14.2 %copy-start.7 = (f32[3,66,32,1]{3,2,1,0:T(8,128)S(1)}, f32[3,66,32,1]{3,2,1,0:T(8,128)}, u32[]{:S(2)}) copy-start(f32[3,66,32,1]{3,2,1,0:T(8,128)} %copy.32) | copy-start | bytes 76036
  39.1 6.6 %collective-permute-start.4 = (f32[3,66,1,130]{3,2,1,0:T(1,128)S(1)}, f32[3,66,1,130]{3,2,1,0:T(1,128)S(1)}, u32[]{:S(2)}, u32[]{:S(2)}) collective-permute-start(f32[3,66,1,130]{3,2,1,0:T(1,128)S(1)} %get-tuple-element.6), channel_id=1, source_target_pairs={{0,1},{1,2},{2,3},{4,5},{5,6},{6,7},{8,9},{9,10},{10,11},{12,13},{... | collective-permute-start | bytes 308888 | tf_op jit(solution)/shard_map/ppermute | solution.py:14
  42.5 7.4 %collective-permute-start.5 = (f32[3,66,1,130]{3,2,1,0:T(1,128)S(1)}, f32[3,66,1,130]{3,2,1,0:T(1,128)S(1)}, u32[]{:S(2)}, u32[]{:S(2)}) collective-permute-start(f32[3,66,1,130]{3,2,1,0:T(1,128)S(1)} %get-tuple-element.7), channel_id=1, source_target_pairs={{1,0},{2,1},{3,2},{5,4},{6,5},{7,6},{9,8},{10,9},{11,10},{13,12},{... | collective-permute-start | bytes 308888 | tf_op jit(solution)/shard_map/ppermute | solution.py:17
  54.4 4.8 %copy-start = (f32[66,34,130]{2,1,0:T(8,128)}, f32[66,34,130]{2,1,0:T(8,128)S(1)}, u32[]{:S(2)}) copy-start(f32[66,34,130]{2,1,0:T(8,128)S(1)} %get-tuple-element.9) | copy-start | bytes 3500644
  54.4 4.8 %copy-start.2 = (f32[66,34,130]{2,1,0:T(8,128)}, f32[66,34,130]{2,1,0:T(8,128)S(1)}, u32[]{:S(2)}) copy-start(f32[66,34,130]{2,1,0:T(8,128)S(1)} %get-tuple-element.10) | copy-start | bytes 3500644
  59.3 12.0 %copy-start.4 = (f32[64,32,128]{2,1,0:T(8,128)}, f32[64,32,128]{2,1,0:T(8,128)S(1)}, u32[]{:S(2)}) copy-start(f32[64,32,128]{2,1,0:T(8,128)S(1)} %sqrt_add_fusion) | copy-start | bytes 3145732
  59.3 12.0 %collective-permute-start.6 = (f32[1,32,128]{2,1,0:T(8,128)S(1)}, f32[1,32,128]{2,1,0:T(8,128)S(1)}, u32[]{:S(2)}, u32[]{:S(2)}) collective-permute-start(f32[1,32,128]{2,1,0:T(8,128)S(1)} %get-tuple-element.20), channel_id=1, source_target_pairs={{16,0},{32,16},{48,32},{64,48},{80,64},{96,80},{112,96},{128,112},... | collective-permute-start | bytes 49160 | tf_op jit(solution)/shard_map/ppermute | solution.py:17
  61.2 10.1 %collective-permute-start.7 = (f32[1,32,128]{2,1,0:T(8,128)S(1)}, f32[1,32,128]{2,1,0:T(8,128)S(1)}, u32[]{:S(2)}, u32[]{:S(2)}) collective-permute-start(f32[1,32,128]{2,1,0:T(8,128)S(1)} %get-tuple-element.19), channel_id=1, source_target_pairs={{0,16},{16,32},{32,48},{48,64},{64,80},{80,96},{96,112},{112,128},... | collective-permute-start | bytes 49160 | tf_op jit(solution)/shard_map/ppermute | solution.py:14
  75.0 7.8 %collective-permute-start.8 = (f32[66,32,1]{0,1,2:T(8,128)S(1)}, f32[66,32,1]{0,1,2:T(8,128)S(1)}, u32[]{:S(2)}, u32[]{:S(2)}) collective-permute-start(f32[66,32,1]{0,1,2:T(8,128)S(1)} %copy.33), channel_id=1, source_target_pairs={{4,0},{8,4},{12,8},{5,1},{9,5},{13,9},{6,2},{10,6},{14,10},{7,3},{... | collective-permute-start | bytes 25352 | tf_op jit(solution)/shard_map/ppermute | solution.py:17
  76.3 17.5 %copy-start.15 = (s32[1,1,1,2]{3,2,1,0:T(1,128)S(1)}, s32[1,1,1,2]{3,2,1,0:T(1,128)}, u32[]{:S(2)}) copy-start(s32[1,1,1,2]{3,2,1,0:T(1,128)} %param.6) | copy-start | bytes 28
  78.2 6.6 %collective-permute-start.9 = (f32[66,32,1]{0,1,2:T(8,128)S(1)}, f32[66,32,1]{0,1,2:T(8,128)S(1)}, u32[]{:S(2)}, u32[]{:S(2)}) collective-permute-start(f32[66,32,1]{0,1,2:T(8,128)S(1)} %copy.35), channel_id=1, source_target_pairs={{0,4},{4,8},{8,12},{1,5},{5,9},{9,13},{2,6},{6,10},{10,14},{3,7},{... | collective-permute-start | bytes 25352 | tf_op jit(solution)/shard_map/ppermute | solution.py:14
  88.5 14.2 %collective-permute-start.10 = (f32[66,1,130]{2,1,0:T(1,128)S(1)}, f32[66,1,130]{2,1,0:T(1,128)S(1)}, u32[]{:S(2)}, u32[]{:S(2)}) collective-permute-start(f32[66,1,130]{2,1,0:T(1,128)S(1)} %get-tuple-element.12), channel_id=1, source_target_pairs={{1,0},{2,1},{3,2},{5,4},{6,5},{7,6},{9,8},{10,9},{11,10},{13,12},{... | collective-permute-start | bytes 102968 | tf_op jit(solution)/shard_map/ppermute | solution.py:17
  89.8 12.9 %collective-permute-start.11 = (f32[66,1,130]{2,1,0:T(1,128)S(1)}, f32[66,1,130]{2,1,0:T(1,128)S(1)}, u32[]{:S(2)}, u32[]{:S(2)}) collective-permute-start(f32[66,1,130]{2,1,0:T(1,128)S(1)} %get-tuple-element.11), channel_id=1, source_target_pairs={{0,1},{1,2},{2,3},{4,5},{5,6},{6,7},{8,9},{9,10},{10,11},{12,13},{... | collective-permute-start | bytes 102968 | tf_op jit(solution)/shard_map/ppermute | solution.py:14
  95.1 39.9 %all-to-all-start = ((f32[16,4,1152]{2,1,0:T(4,128)}), f32[16,4,1152]{2,1,0:T(4,128)S(1)}, u32[]{:S(2)}, u32[]{:S(2)}) async-start(f32[16,4,1152]{2,1,0:T(4,128)} %copy.40), calls=%async_computation | async-start | bytes 589824 | tf_op jit(solution)/shard_map/all_to_all | solution.py:98
  102.7 18.0 %copy-start.1 = (f32[66,34,130]{2,1,0:T(8,128)S(1)}, f32[66,34,130]{2,1,0:T(8,128)}, u32[]{:S(2)}) copy-start(f32[66,34,130]{2,1,0:T(8,128)} %copy-done) | copy-start | bytes 3500644
  102.7 18.0 %copy-start.3 = (f32[66,34,130]{2,1,0:T(8,128)S(1)}, f32[66,34,130]{2,1,0:T(8,128)}, u32[]{:S(2)}) copy-start(f32[66,34,130]{2,1,0:T(8,128)} %copy-done.2) | copy-start | bytes 3500644
  102.7 18.0 %copy-start.5 = (f32[64,32,128]{2,1,0:T(8,128)S(1)}, f32[64,32,128]{2,1,0:T(8,128)}, u32[]{:S(2)}) copy-start(f32[64,32,128]{2,1,0:T(8,128)} %copy-done.4) | copy-start | bytes 3145732
  102.7 18.0 %copy-start.8 = (f32[66,32,1]{2,1,0:T(8,128)S(1)}, f32[66,32,1]{2,1,0:T(8,128)}, u32[]{:S(2)}) copy-start(f32[66,32,1]{2,1,0:T(8,128)} %copy.34) | copy-start | bytes 25348
  102.7 18.0 %copy-start.9 = (f32[66,32,1]{2,1,0:T(8,128)S(1)}, f32[66,32,1]{2,1,0:T(8,128)}, u32[]{:S(2)}) copy-start(f32[66,32,1]{2,1,0:T(8,128)} %copy.36) | copy-start | bytes 25348
  227.6 4.0 %copy-start.14 = (f32[64,1152]{1,0:T(8,128)}, f32[64,1152]{1,0:T(8,128)S(1)}, u32[]{:S(2)}) copy-start(f32[64,1152]{1,0:T(8,128)S(1)} %reshape.53) | copy-start | bytes 884740
  233.1 1.2 copy-start.11
  233.2 1.5 copy-start.12
  233.2 1.8 copy-start.13
where the time goes:
time: 238 us; the launch traced here: 237 us
  blocking collectives  91.7 us (39%)
  other arithmetic  49.5 us (21%)
  starting transfers between devices  42.1 us (18%)
  local copies, waits for them, and re-layouts  35.2 us (15%)
  matrix products  11.5 us (5%)
  waiting for transfers between devices  6.24 us (3%)
    psum x1, blocking collectives, body(): owned = lax.psum(jnp.sum(received, axis=0), ('gy', 'gz'))  59.5 us
    all_gather x1, blocking collectives, body(): lax.all_gather(actuate(owned, owned_coef), 'gx', axis=0, tiled=True)  32.2 us
    another operation x3, other arithmetic, advance(): return jnp.stack(result)  32.2 us
    ppermute x6, starting transfers between devices, padded_2(): lax.ppermute(lax.slice_in_dim(block, block.shape[dim] - width, None, axis...  25.5 us
    slice x5, local copies, waits for them, and re-layouts, padded_2(): lax.slice_in_dim(block, block.shape[dim] - width, None, axis=dim)  10.3 us
    ppermute x6, starting transfers between devices, padded_2(): lax.ppermute(lax.slice_in_dim(block, 0, width, axis=dim), axis, backward)  8.99 us
    all_to_all x1, starting transfers between devices, body(): lax.all_to_all(partial_sample.reshape(rows, per_row, -1), 'gx', split_axi...  7.6 us
    concatenate x3, other arithmetic, padded_2(): block = jnp.concatenate([low, block, high], axis=dim)  5.95 us
  transfers between devices with their start and end apart: 13, of which 3 were waited for; matrix products, arithmetic and copies ran while one was open for 23% of the time, Pallas kernels for 0%

commit v1 on v0

--- a/solution.py
+++ b/solution.py
@@ -98,7 +98,7 @@
     received = lax.all_to_all(
         partial_sample.reshape(rows, per_row, -1), "gx", split_axis=0, concat_axis=0, tiled=True
     )
-    owned = lax.psum(jnp.sum(received, axis=0), ("gy", "gz"))
+    owned = jnp.sum(lax.all_gather(jnp.sum(received, axis=0), ("gy", "gz")), axis=0)
     owned_coef = lax.dynamic_slice_in_dim(chord, lax.axis_index("gx") * per_row, per_row, 0)
     forces = lax.all_gather(actuate(owned, owned_coef), "gx", axis=0, tiled=True)
     tile_force = jnp.dot(owning_block, forces, precision=lax.Precision.HIGHEST).astype(jnp.bfloat16)

time: 238 us -> 190 us (0.80)
  blocking collectives: 91.7 us -> 43.1 us
    psum x1 -> x0, blocking collectives: 59.5 us -> none  [body(): owned = lax.psum(jnp.sum(received, axis=0), ('gy', 'gz'))]
    all_gather x0 -> x1, blocking collectives: none -> 19.7 us  [body(): lax.all_gather(jnp.sum(received, axis=0), ('gy', 'gz'))]
    all_gather x1, blocking collectives: 32.2 us -> 23.4 us  [body(): lax.all_gather(actuate(owned, owned_coef), 'gx', axis=0, tiled=True)]
  transfers between devices with their start and end apart: 13 -> 13, of which waited for: 3 -> 3; matrix products, arithmetic and copies ran while one was open for 23% -> 29% of each run, Pallas kernels for 0% -> 0%
where the time goes in v1:
time: 190 us; the launch traced here: 189 us
  other arithmetic  49.6 us (26%)
  blocking collectives  43.1 us (23%)
  starting transfers between devices  42.1 us (22%)
  local copies, waits for them, and re-layouts  35.2 us (19%)
  matrix products  11.5 us (6%)
  waiting for transfers between devices  6.24 us (3%)
    another operation x3, other arithmetic, advance(): return jnp.stack(result)  32.2 us
    ppermute x6, starting transfers between devices, padded_2(): lax.ppermute(lax.slice_in_dim(block, block.shape[dim] - width, None, axis...  25.5 us
    all_gather x1, blocking collectives, body(): lax.all_gather(actuate(owned, owned_coef), 'gx', axis=0, tiled=True)  23.4 us
    all_gather x1, blocking collectives, body(): lax.all_gather(jnp.sum(received, axis=0), ('gy', 'gz'))  19.7 us
    slice x5, local copies, waits for them, and re-layouts, padded_2(): lax.slice_in_dim(block, block.shape[dim] - width, None, axis=dim)  10.3 us
    ppermute x6, starting transfers between devices, padded_2(): lax.ppermute(lax.slice_in_dim(block, 0, width, axis=dim), axis, backward)  8.99 us
    all_to_all x1, starting transfers between devices, body(): lax.all_to_all(partial_sample.reshape(rows, per_row, -1), 'gx', split_axi...  7.6 us
    concatenate x3, other arithmetic, padded_2(): block = jnp.concatenate([low, block, high], axis=dim)  5.95 us
  transfers between devices with their start and end apart: 13, of which 3 were waited for; matrix products, arithmetic and copies ran while one was open for 29% of the time, Pallas kernels for 0%

profile of v1, /device:TPU:1, one launch (start us, length us, event | category | flops | bytes accessed | tf_op | source)
XLA Modules:
  0.0 188.9 jit_solution(7824118150780139517)
XLA Ops:
  0.6 0.8 fusion.31
  1.5 4.9 %collective-permute-start = (f32[3,1,32,128]{3,2,1,0:T(8,128)S(1)}, f32[3,1,32,128]{3,2,1,0:T(8,128)S(1)}, u32[]{:S(2)}, u32[]{:S(2)}) collective-permute-start(f32[3,1,32,128]{3,2,1,0:T(8,128)S(1)} %get-tuple-element.16), channel_id=1, source_target_pairs={{0,16},{16,32},{32,48},{48,64},{64,80},{80,96},{96,112},{112,128},... | collective-permute-start | bytes 147464 | tf_op jit(solution)/shard_map/ppermute | solution.py:14
  6.4 1.9 %collective-permute-start.1 = (f32[3,1,32,128]{3,2,1,0:T(8,128)S(1)}, f32[3,1,32,128]{3,2,1,0:T(8,128)S(1)}, u32[]{:S(2)}, u32[]{:S(2)}) collective-permute-start(f32[3,1,32,128]{3,2,1,0:T(8,128)S(1)} %get-tuple-element.15), channel_id=1, source_target_pairs={{16,0},{32,16},{48,32},{64,48},{80,64},{96,80},{112,96},{128,112},... | collective-permute-start | bytes 147464 | tf_op jit(solution)/shard_map/ppermute | solution.py:17
  8.3 2.2 %constant_dynamic-update-slice_fusion.1 = f32[3,66,32,128]{3,2,1,0:T(8,128)S(1)} fusion(f32[3,66,32,128]{3,2,1,0:T(8,128)S(1)} %constant_dynamic-update-slice_fusion.2, f32[3,64,32,128]{3,2,1,0:T(8,128)} %param.5), kind=kLoop, calls=%fused_computation.71 | loop fusion | bytes 6291456
  10.5 1.3 collective-permute-done.1
  11.8 3.9 %fusion.30 = (f32[3,66,32,1]{3,2,1,0:T(8,128)}, f32[3,66,32,1]{3,2,1,0:T(8,128)}) fusion(f32[3,66,32,128]{3,2,1,0:T(8,128)S(1)} %constant_dynamic-update-slice_fusion), kind=kLoop, calls=%fused_computation.87 | loop fusion | bytes 101376 | tf_op jit(solution)/shard_map/slice | solution.py:15
  15.7 2.8 %copy.29 = f32[3,66,32,1]{1,2,3,0:T(8,128)S(1)} copy(f32[3,66,32,1]{3,2,1,0:T(8,128)} %get-tuple-element.13) | data formatting | bytes 50688 | tf_op jit(solution)/shard_map/slice | solution.py:15
  18.5 3.1 %collective-permute-start.2 = (f32[3,66,32,1]{1,2,3,0:T(8,128)S(1)}, f32[3,66,32,1]{1,2,3,0:T(8,128)S(1)}, u32[]{:S(2)}, u32[]{:S(2)}) collective-permute-start(f32[3,66,32,1]{1,2,3,0:T(8,128)S(1)} %copy.29), channel_id=1, source_target_pairs={{0,4},{4,8},{8,12},{1,5},{5,9},{9,13},{2,6},{6,10},{10,14},{3,7},{... | collective-permute-start | bytes 76040 | tf_op jit(solution)/shard_map/ppermute | solution.py:14
  21.6 2.8 %copy.30 = f32[3,66,32,1]{1,2,3,0:T(8,128)S(1)} copy(f32[3,66,32,1]{3,2,1,0:T(8,128)} %get-tuple-element.14) | data formatting | bytes 50688 | tf_op jit(solution)/shard_map/slice | solution.py:17
  24.4 1.3 collective-permute-start.3
  25.7 4.6 %reshape.47 = f32[3,64,4096]{2,1,0:T(8,128)} reshape(f32[3,64,32,128]{3,2,1,0:T(8,128)} %param.5) | data formatting | bytes 6291456 | tf_op jit(solution)/shard_map/reshape | solution.py:79
  30.3 2.7 %copy.31 = f32[3,66,32,1]{3,2,1,0:T(8,128)} copy(f32[3,66,32,1]{1,2,3,0:T(8,128)S(1)} %collective-permute-done.2) | data formatting | bytes 50688 | tf_op jit(solution)/shard_map/ppermute | solution.py:14
  33.0 2.7 %copy.32 = f32[3,66,32,1]{3,2,1,0:T(8,128)} copy(f32[3,66,32,1]{1,2,3,0:T(8,128)S(1)} %collective-permute-done.3) | data formatting | bytes 50688 | tf_op jit(solution)/shard_map/ppermute | solution.py:17
  35.7 3.4 %pad_maximum_fusion.22 = (f32[3,66,1,130]{3,2,1,0:T(1,128)S(1)}, f32[3,66,1,130]{3,2,1,0:T(1,128)S(1)}) fusion(f32[3,66,32,1]{3,2,1,0:T(8,128)} %copy.32, f32[3,66,32,128]{3,2,1,0:T(8,128)S(1)} %constant_dynamic-update-slice_fusion, f32[3,66,32,1]{3,2,1,0:T(8,128)} %copy.31), kind=kLoop, calls=%fused_computation.60 | loop fusion | flops 102960 | bytes 3500640 | tf_op jit(solution)/shard_map/slice | solution.py:15
  39.1 3.3 %collective-permute-start.4 = (f32[3,66,1,130]{3,2,1,0:T(1,128)S(1)}, f32[3,66,1,130]{3,2,1,0:T(1,128)S(1)}, u32[]{:S(2)}, u32[]{:S(2)}) collective-permute-start(f32[3,66,1,130]{3,2,1,0:T(1,128)S(1)} %get-tuple-element.6), channel_id=1, source_target_pairs={{0,1},{1,2},{2,3},{4,5},{5,6},{6,7},{8,9},{9,10},{10,11},{12,13},{... | collective-permute-start | bytes 308888 | tf_op jit(solution)/shard_map/ppermute | solution.py:14
  42.5 1.3 collective-permute-start.5
  43.8 1.1 convolution_convert_fusion
  44.9 0.9 collective-permute-done.4
  45.8 4.1 %collective-permute-done.5 = f32[3,66,1,130]{3,2,1,0:T(1,128)S(1)} collective-permute-done((f32[3,66,1,130]{3,2,1,0:T(1,128)S(1)}, f32[3,66,1,130]{3,2,1,0:T(1,128)S(1)}, u32[]{:S(2)}, u32[]{:S(2)}) %collective-permute-start.5) | collective-permute-done | bytes 102992 | tf_op jit(solution)/shard_map/ppermute | solution.py:17
  49.9 4.0 %pad_maximum_fusion = f32[3,66,34,130]{3,2,1,0:T(8,128)S(1)} fusion(f32[3,66,1,130]{3,2,1,0:T(1,128)S(1)} %collective-permute-done.5, f32[3,66,32,1]{3,2,1,0:T(8,128)S(1)} %copy-done.7, f32[3,66,32,128]{3,2,1,0:T(8,128)S(1)} %constant_dynamic-update-slice_fusion, f32[3,66,32,1]{3,2,1,0:T(8,128)S(1)} %copy-done.6, f32[3,66,1,130]{3,2,1,0:T(1,128)S(1)} %collective-permute-done.4), kind=kLoop, calls=%fused_computation | loop fusion | flops 3500640 | bytes 7001280 | tf_op jit(solution)/shard_map/concatenate | solution.py:18
  53.9 0.5 slice_bitcast_fusion.1
  54.5 4.8 %sqrt_add_fusion = f32[64,32,128]{2,1,0:T(8,128)S(1)} fusion(f32[66,34,130]{2,1,0:T(8,128)S(1)} %get-tuple-element.10, f32[66,34,130]{2,1,0:T(8,128)S(1)} %get-tuple-element.8, f32[66,34,130]{2,1,0:T(8,128)S(1)} %get-tuple-element.9), kind=kLoop, calls=%fused_computation.45 | loop fusion | flops 9961472 | bytes 19922944 | tf_op jit(solution)/shard_map/add | solution.py:39
  59.3 1.9 %collective-permute-start.6 = (f32[1,32,128]{2,1,0:T(8,128)S(1)}, f32[1,32,128]{2,1,0:T(8,128)S(1)}, u32[]{:S(2)}, u32[]{:S(2)}) collective-permute-start(f32[1,32,128]{2,1,0:T(8,128)S(1)} %get-tuple-element.20), channel_id=1, source_target_pairs={{16,0},{32,16},{48,32},{64,48},{80,64},{96,80},{112,96},{128,112},... | collective-permute-start | bytes 49160 | tf_op jit(solution)/shard_map/ppermute | solution.py:17
  61.2 5.5 %collective-permute-start.7 = (f32[1,32,128]{2,1,0:T(8,128)S(1)}, f32[1,32,128]{2,1,0:T(8,128)S(1)}, u32[]{:S(2)}, u32[]{:S(2)}) collective-permute-start(f32[1,32,128]{2,1,0:T(8,128)S(1)} %get-tuple-element.19), channel_id=1, source_target_pairs={{0,16},{16,32},{32,48},{48,64},{64,80},{80,96},{96,112},{112,128},... | collective-permute-start | bytes 49160 | tf_op jit(solution)/shard_map/ppermute | solution.py:14
  66.8 4.5 %fusion.2 = f32[2,3,384]{2,1,0:T(4,128)S(1)} fusion(bf16[1,1,1,2,384,4096]{5,4,3,2,1,0:T(8,128)(2,1)} %param.8, bf16[2,3,4096]{2,0,1:T(2,128)(2,1)S(1)} %convolution_convert_fusion), kind=kOutput, calls=%fused_computation.3 | convolution fusion | flops 18874368 | bytes 6349824 | tf_op jit(solution)/shard_map/spq,scq->scp/dot_general | solution.py:84
  71.4 1.7 fusion.32
  73.1 1.9 copy.33
  75.0 1.3 collective-permute-start.8
  76.3 1.9 copy.35
  78.2 4.6 %collective-permute-start.9 = (f32[66,32,1]{0,1,2:T(8,128)S(1)}, f32[66,32,1]{0,1,2:T(8,128)S(1)}, u32[]{:S(2)}, u32[]{:S(2)}) collective-permute-start(f32[66,32,1]{0,1,2:T(8,128)S(1)} %copy.35), channel_id=1, source_target_pairs={{0,4},{4,8},{8,12},{1,5},{5,9},{9,13},{2,6},{6,10},{10,14},{3,7},{... | collective-permute-start | bytes 25352 | tf_op jit(solution)/shard_map/ppermute | solution.py:14
  82.8 1.9 %copy.34 = f32[66,32,1]{2,1,0:T(8,128)} copy(f32[66,32,1]{0,1,2:T(8,128)S(1)} %collective-permute-done.8) | data formatting | bytes 16896 | tf_op jit(solution)/shard_map/ppermute | solution.py:17
  84.7 1.9 %copy.36 = f32[66,32,1]{2,1,0:T(8,128)} copy(f32[66,32,1]{0,1,2:T(8,128)S(1)} %collective-permute-done.9) | data formatting | bytes 16896 | tf_op jit(solution)/shard_map/ppermute | solution.py:14
  86.6 1.9 pad_maximum_fusion.23
  88.5 1.3 collective-permute-start.10
  89.8 4.0 %collective-permute-start.11 = (f32[66,1,130]{2,1,0:T(1,128)S(1)}, f32[66,1,130]{2,1,0:T(1,128)S(1)}, u32[]{:S(2)}, u32[]{:S(2)}) collective-permute-start(f32[66,1,130]{2,1,0:T(1,128)S(1)} %get-tuple-element.11), channel_id=1, source_target_pairs={{0,1},{1,2},{2,3},{4,5},{5,6},{6,7},{8,9},{9,10},{10,11},{12,13},{... | collective-permute-start | bytes 102968 | tf_op jit(solution)/shard_map/ppermute | solution.py:14
  94.2 0.8 copy.40
  95.1 7.6 %all-to-all-start = ((f32[16,4,1152]{2,1,0:T(4,128)}), f32[16,4,1152]{2,1,0:T(4,128)S(1)}, u32[]{:S(2)}, u32[]{:S(2)}) async-start(f32[16,4,1152]{2,1,0:T(4,128)} %copy.40), calls=%async_computation | async-start | bytes 589824 | tf_op jit(solution)/shard_map/all_to_all | solution.py:98
  102.7 17.9 %add_bitcast_fusion.2 = f32[1,64,32,128]{3,2,1,0:T(8,128)} fusion(f32[66,34,130]{2,1,0:T(8,128)} %copy-done.2, f32[66,34,130]{2,1,0:T(8,128)S(1)} %get-tuple-element.8, f32[66,34,130]{2,1,0:T(8,128)} %copy-done, f32[64,32,128]{2,1,0:T(8,128)} %copy-done.4, f32[1,32,128]{2,1,0:T(8,128)S(1)} %collective-permute-done.6, ...), kind=kLoop, calls=%fused_computation.44 | loop fusion | flops 15990784 | bytes 11652640 | tf_op jit(solution)/shard_map/stack | solution.py:57
  120.7 7.1 %add_bitcast_fusion.1 = f32[1,64,32,128]{3,2,1,0:T(8,128)} fusion(f32[66,34,130]{2,1,0:T(8,128)S(1)} %get-tuple-element.8, f32[66,34,130]{2,1,0:T(8,128)S(1)} %copy-done.3, f32[66,34,130]{2,1,0:T(8,128)S(1)} %copy-done.1, f32[64,32,128]{2,1,0:T(8,128)S(1)} %copy-done.5, f32[1,32,128]{2,1,0:T(8,128)S(1)} %collective-permute-done.6, ...), kind=kLoop, calls=%fused_computation.43 | loop fusion | flops 15990784 | bytes 11652640 | tf_op jit(solution)/shard_map/stack | solution.py:57
  127.9 7.1 %add_bitcast_fusion = f32[1,64,32,128]{3,2,1,0:T(8,128)} fusion(f32[66,34,130]{2,1,0:T(8,128)S(1)} %copy-done.1, f32[66,34,130]{2,1,0:T(8,128)S(1)} %copy-done.3, f32[66,34,130]{2,1,0:T(8,128)S(1)} %get-tuple-element.8, f32[64,32,128]{2,1,0:T(8,128)S(1)} %copy-done.5, f32[1,32,128]{2,1,0:T(8,128)S(1)} %collective-permute-done.6, ...), kind=kLoop, calls=%fused_computation.42 | loop fusion | flops 15990784 | bytes 11652640 | tf_op jit(solution)/shard_map/stack | solution.py:57
  135.0 19.7 %all-gather.1 = f32[16,4,1152]{2,1,0:T(4,128)S(1)} all-gather(f32[1,4,1152]{2,1,0:T(4,128)S(1)} %bitcast.44), channel_id=2, replica_groups=mesh['gx'=16,'gy'=4,'gz'=4] {'gy','gz'}, dimensions={0}, use_global_device_ids=true | all-gather | bytes 313344 | tf_op jit(solution)/shard_map/all_gather | solution.py:101
  154.8 0.7 sqrt_multiply_fusion
  155.6 23.4 %all-gather.2 = f32[16,4,1152]{2,1,0:T(4,128)S(1)} all-gather(f32[1,4,1152]{2,1,0:T(4,128)S(1)} %multiply_bitcast_fusion), channel_id=1, replica_groups=mesh['gx'=16,'gy'=4,'gz'=4] {'gx'}, dimensions={0}, use_global_device_ids=true | all-gather | bytes 313344 | tf_op jit(solution)/shard_map/all_gather | solution.py:103
  179.3 3.7 %fusion = f32[2,3,4096]{2,1,0:T(4,128)S(1)} fusion(bf16[2,3,384]{2,1,0:T(4,128)(2,1)S(1)} %reshape.50, bf16[1,1,1,2,384,4096]{5,4,3,2,1,0:T(8,128)(2,1)} %param.8), kind=kOutput, calls=%fused_computation.1 | convolution fusion | flops 18874368 | bytes 6394368 | tf_op jit(solution)/shard_map/axz,ahx->ahz/dot_general | solution.py:105
  183.1 1.5 fusion.16
  184.6 0.5 copy.42
  185.2 0.6 copy-done.11
  186.4 2.4 %bitcast_add_fusion = f32[3,64,32,128]{3,2,1,0:T(8,128)} fusion(f32[1,64,32,128]{3,2,1,0:T(8,128)S(1)} %copy-done.13, f32[1,64,32,128]{3,2,1,0:T(8,128)S(1)} %copy-done.12, f32[1,64,32,128]{3,2,1,0:T(8,128)S(1)} %copy-done.11, f32[3,64,32,128]{3,2,1,0:T(8,128)S(1)} %bitcast.43), kind=kLoop, calls=%fused_computation.6 | loop fusion | flops 2359296 | bytes 9437184 | tf_op jit(solution)/shard_map/add | solution.py:117
  (59 shorter events, 1.8 us)
Async XLA Ops:
  1.5 6.9 %collective-permute-start = (f32[3,1,32,128]{3,2,1,0:T(8,128)S(1)}, f32[3,1,32,128]{3,2,1,0:T(8,128)S(1)}, u32[]{:S(2)}, u32[]{:S(2)}) collective-permute-start(f32[3,1,32,128]{3,2,1,0:T(8,128)S(1)} %get-tuple-element.16), channel_id=1, source_target_pairs={{0,16},{16,32},{32,48},{48,64},{64,80},{80,96},{96,112},{112,128},... | collective-permute-start | bytes 147464 | tf_op jit(solution)/shard_map/ppermute | solution.py:14
  6.4 5.4 %collective-permute-start.1 = (f32[3,1,32,128]{3,2,1,0:T(8,128)S(1)}, f32[3,1,32,128]{3,2,1,0:T(8,128)S(1)}, u32[]{:S(2)}, u32[]{:S(2)}) collective-permute-start(f32[3,1,32,128]{3,2,1,0:T(8,128)S(1)} %get-tuple-element.15), channel_id=1, source_target_pairs={{16,0},{32,16},{48,32},{64,48},{80,64},{96,80},{112,96},{128,112},... | collective-permute-start | bytes 147464 | tf_op jit(solution)/shard_map/ppermute | solution.py:17
  18.5 11.8 %collective-permute-start.2 = (f32[3,66,32,1]{1,2,3,0:T(8,128)S(1)}, f32[3,66,32,1]{1,2,3,0:T(8,128)S(1)}, u32[]{:S(2)}, u32[]{:S(2)}) collective-permute-start(f32[3,66,32,1]{1,2,3,0:T(8,128)S(1)} %copy.29), channel_id=1, source_target_pairs={{0,4},{4,8},{8,12},{1,5},{5,9},{9,13},{2,6},{6,10},{10,14},{3,7},{... | collective-permute-start | bytes 76040 | tf_op jit(solution)/shard_map/ppermute | solution.py:14
  24.4 8.6 %collective-permute-start.3 = (f32[3,66,32,1]{1,2,3,0:T(8,128)S(1)}, f32[3,66,32,1]{1,2,3,0:T(8,128)S(1)}, u32[]{:S(2)}, u32[]{:S(2)}) collective-permute-start(f32[3,66,32,1]{1,2,3,0:T(8,128)S(1)} %copy.30), channel_id=1, source_target_pairs={{4,0},{8,4},{12,8},{5,1},{9,5},{13,9},{6,2},{10,6},{14,10},{7,3},{... | collective-permute-start | bytes 76040 | tf_op jit(solution)/shard_map/ppermute | solution.py:17
  35.7 8.1 %copy-start.10 = (f32[3,64,4096]{2,1,0:T(8,128)S(1)}, f32[3,64,4096]{2,1,0:T(8,128)}, u32[]{:S(2)}) copy-start(f32[3,64,4096]{2,1,0:T(8,128)} %reshape.47) | copy-start | bytes 9437188
  35.7 8.1 %copy-start.16 = (s32[1,1,1,2]{3,2,1,0:T(1,128)S(1)}, s32[1,1,1,2]{3,2,1,0:T(1,128)}, u32[]{:S(2)}) copy-start(s32[1,1,1,2]{3,2,1,0:T(1,128)} %param.7) | copy-start | bytes 28
  35.7 14.2 %copy-start.6 = (f32[3,66,32,1]{3,2,1,0:T(8,128)S(1)}, f32[3,66,32,1]{3,2,1,0:T(8,128)}, u32[]{:S(2)}) copy-start(f32[3,66,32,1]{3,2,1,0:T(8,128)} %copy.31) | copy-start | bytes 76036
  35.7 14.2 %copy-start.7 = (f32[3,66,32,1]{3,2,1,0:T(8,128)S(1)}, f32[3,66,32,1]{3,2,1,0:T(8,128)}, u32[]{:S(2)}) copy-start(f32[3,66,32,1]{3,2,1,0:T(8,128)} %copy.32) | copy-start | bytes 76036
  39.1 6.6 %collective-permute-start.4 = (f32[3,66,1,130]{3,2,1,0:T(1,128)S(1)}, f32[3,66,1,130]{3,2,1,0:T(1,128)S(1)}, u32[]{:S(2)}, u32[]{:S(2)}) collective-permute-start(f32[3,66,1,130]{3,2,1,0:T(1,128)S(1)} %get-tuple-element.6), channel_id=1, source_target_pairs={{0,1},{1,2},{2,3},{4,5},{5,6},{6,7},{8,9},{9,10},{10,11},{12,13},{... | collective-permute-start | bytes 308888 | tf_op jit(solution)/shard_map/ppermute | solution.py:14
  42.5 7.4 %collective-permute-start.5 = (f32[3,66,1,130]{3,2,1,0:T(1,128)S(1)}, f32[3,66,1,130]{3,2,1,0:T(1,128)S(1)}, u32[]{:S(2)}, u32[]{:S(2)}) collective-permute-start(f32[3,66,1,130]{3,2,1,0:T(1,128)S(1)} %get-tuple-element.7), channel_id=1, source_target_pairs={{1,0},{2,1},{3,2},{5,4},{6,5},{7,6},{9,8},{10,9},{11,10},{13,12},{... | collective-permute-start | bytes 308888 | tf_op jit(solution)/shard_map/ppermute | solution.py:17
  54.4 4.8 %copy-start = (f32[66,34,130]{2,1,0:T(8,128)}, f32[66,34,130]{2,1,0:T(8,128)S(1)}, u32[]{:S(2)}) copy-start(f32[66,34,130]{2,1,0:T(8,128)S(1)} %get-tuple-element.9) | copy-start | bytes 3500644
  54.4 4.8 %copy-start.2 = (f32[66,34,130]{2,1,0:T(8,128)}, f32[66,34,130]{2,1,0:T(8,128)S(1)}, u32[]{:S(2)}) copy-start(f32[66,34,130]{2,1,0:T(8,128)S(1)} %get-tuple-element.10) | copy-start | bytes 3500644
  59.3 12.0 %copy-start.4 = (f32[64,32,128]{2,1,0:T(8,128)}, f32[64,32,128]{2,1,0:T(8,128)S(1)}, u32[]{:S(2)}) copy-start(f32[64,32,128]{2,1,0:T(8,128)S(1)} %sqrt_add_fusion) | copy-start | bytes 3145732
  59.3 12.0 %collective-permute-start.6 = (f32[1,32,128]{2,1,0:T(8,128)S(1)}, f32[1,32,128]{2,1,0:T(8,128)S(1)}, u32[]{:S(2)}, u32[]{:S(2)}) collective-permute-start(f32[1,32,128]{2,1,0:T(8,128)S(1)} %get-tuple-element.20), channel_id=1, source_target_pairs={{16,0},{32,16},{48,32},{64,48},{80,64},{96,80},{112,96},{128,112},... | collective-permute-start | bytes 49160 | tf_op jit(solution)/shard_map/ppermute | solution.py:17
  61.2 10.1 %collective-permute-start.7 = (f32[1,32,128]{2,1,0:T(8,128)S(1)}, f32[1,32,128]{2,1,0:T(8,128)S(1)}, u32[]{:S(2)}, u32[]{:S(2)}) collective-permute-start(f32[1,32,128]{2,1,0:T(8,128)S(1)} %get-tuple-element.19), channel_id=1, source_target_pairs={{0,16},{16,32},{32,48},{48,64},{64,80},{80,96},{96,112},{112,128},... | collective-permute-start | bytes 49160 | tf_op jit(solution)/shard_map/ppermute | solution.py:14
  75.0 7.8 %collective-permute-start.8 = (f32[66,32,1]{0,1,2:T(8,128)S(1)}, f32[66,32,1]{0,1,2:T(8,128)S(1)}, u32[]{:S(2)}, u32[]{:S(2)}) collective-permute-start(f32[66,32,1]{0,1,2:T(8,128)S(1)} %copy.33), channel_id=1, source_target_pairs={{4,0},{8,4},{12,8},{5,1},{9,5},{13,9},{6,2},{10,6},{14,10},{7,3},{... | collective-permute-start | bytes 25352 | tf_op jit(solution)/shard_map/ppermute | solution.py:17
  76.3 17.5 %copy-start.15 = (s32[1,1,1,2]{3,2,1,0:T(1,128)S(1)}, s32[1,1,1,2]{3,2,1,0:T(1,128)}, u32[]{:S(2)}) copy-start(s32[1,1,1,2]{3,2,1,0:T(1,128)} %param.6) | copy-start | bytes 28
  78.2 6.6 %collective-permute-start.9 = (f32[66,32,1]{0,1,2:T(8,128)S(1)}, f32[66,32,1]{0,1,2:T(8,128)S(1)}, u32[]{:S(2)}, u32[]{:S(2)}) collective-permute-start(f32[66,32,1]{0,1,2:T(8,128)S(1)} %copy.35), channel_id=1, source_target_pairs={{0,4},{4,8},{8,12},{1,5},{5,9},{9,13},{2,6},{6,10},{10,14},{3,7},{... | collective-permute-start | bytes 25352 | tf_op jit(solution)/shard_map/ppermute | solution.py:14
  88.5 14.2 %collective-permute-start.10 = (f32[66,1,130]{2,1,0:T(1,128)S(1)}, f32[66,1,130]{2,1,0:T(1,128)S(1)}, u32[]{:S(2)}, u32[]{:S(2)}) collective-permute-start(f32[66,1,130]{2,1,0:T(1,128)S(1)} %get-tuple-element.12), channel_id=1, source_target_pairs={{1,0},{2,1},{3,2},{5,4},{6,5},{7,6},{9,8},{10,9},{11,10},{13,12},{... | collective-permute-start | bytes 102968 | tf_op jit(solution)/shard_map/ppermute | solution.py:17
  89.8 12.9 %collective-permute-start.11 = (f32[66,1,130]{2,1,0:T(1,128)S(1)}, f32[66,1,130]{2,1,0:T(1,128)S(1)}, u32[]{:S(2)}, u32[]{:S(2)}) collective-permute-start(f32[66,1,130]{2,1,0:T(1,128)S(1)} %get-tuple-element.11), channel_id=1, source_target_pairs={{0,1},{1,2},{2,3},{4,5},{5,6},{6,7},{8,9},{9,10},{10,11},{12,13},{... | collective-permute-start | bytes 102968 | tf_op jit(solution)/shard_map/ppermute | solution.py:14
  95.1 39.9 %all-to-all-start = ((f32[16,4,1152]{2,1,0:T(4,128)}), f32[16,4,1152]{2,1,0:T(4,128)S(1)}, u32[]{:S(2)}, u32[]{:S(2)}) async-start(f32[16,4,1152]{2,1,0:T(4,128)} %copy.40), calls=%async_computation | async-start | bytes 589824 | tf_op jit(solution)/shard_map/all_to_all | solution.py:98
  102.7 18.0 %copy-start.1 = (f32[66,34,130]{2,1,0:T(8,128)S(1)}, f32[66,34,130]{2,1,0:T(8,128)}, u32[]{:S(2)}) copy-start(f32[66,34,130]{2,1,0:T(8,128)} %copy-done) | copy-start | bytes 3500644
  102.7 18.0 %copy-start.3 = (f32[66,34,130]{2,1,0:T(8,128)S(1)}, f32[66,34,130]{2,1,0:T(8,128)}, u32[]{:S(2)}) copy-start(f32[66,34,130]{2,1,0:T(8,128)} %copy-done.2) | copy-start | bytes 3500644
  102.7 18.0 %copy-start.5 = (f32[64,32,128]{2,1,0:T(8,128)S(1)}, f32[64,32,128]{2,1,0:T(8,128)}, u32[]{:S(2)}) copy-start(f32[64,32,128]{2,1,0:T(8,128)} %copy-done.4) | copy-start | bytes 3145732
  102.7 18.0 %copy-start.8 = (f32[66,32,1]{2,1,0:T(8,128)S(1)}, f32[66,32,1]{2,1,0:T(8,128)}, u32[]{:S(2)}) copy-start(f32[66,32,1]{2,1,0:T(8,128)} %copy.34) | copy-start | bytes 25348
  102.7 18.0 %copy-start.9 = (f32[66,32,1]{2,1,0:T(8,128)S(1)}, f32[66,32,1]{2,1,0:T(8,128)}, u32[]{:S(2)}) copy-start(f32[66,32,1]{2,1,0:T(8,128)} %copy.36) | copy-start | bytes 25348
  179.1 4.0 %copy-start.14 = (f32[64,1152]{1,0:T(8,128)}, f32[64,1152]{1,0:T(8,128)S(1)}, u32[]{:S(2)}) copy-start(f32[64,1152]{1,0:T(8,128)S(1)} %reshape.56) | copy-start | bytes 884740
  184.6 1.2 copy-start.11
  184.6 1.5 copy-start.12
  184.6 1.8 copy-start.13
